TPU v7x, 128 devices: a whole 4x4x4 slice. The times are simulated.
128 devices in a mesh: dp: 8 (over y, x_lo), tp: 16 (over z, x_hi, core).
Axes of the slice: x: 4 (x_hi: 2, x_lo: 2; x = x_hi * 2 + x_lo), y: 4, z: 4, core: 2. Of those that a mesh axis runs over, the one named last changes fastest.
Arguments:
- gradients: bfloat16 [8, 4, 3072, 768], P('dp', None, 'tp'), may hold values from -6 to 6, as said below
- right_factor: float32 [4, 768, 8], replicated, may hold values from -6 to 6
- weights_before: float32 [4, 3072, 768], P(None, 'tp', 'dp'), may hold values from -0.21875 to 0.21875
- momentum: float32 [4, 3072, 768], P(None, 'tp', 'dp'), may hold values from -0.3125 to 0.3125
Outputs:
- new_weights: float32 [4, 3072, 768], P(None, 'tp', 'dp')
- new_basis: float32 [4, 768, 8], replicated
- new_momentum: float32 [4, 3072, 768], P(None, 'tp', 'dp')
Inputs may be any that keep to these rules, and one draw needn't show every extreme that they name: gradients holds numbers from -6 to 6.
All inputs are finite; a program needn't handle non-finite values.
Results may differ from a plain program's by a relative error of at most 0.0003.
Values sent between devices are 32-bit elements.
A program may use at most 64 MiB of HBM per device.

v0:
```python
import jax
import jax.numpy as jnp
from jax import lax
from jax.sharding import Mesh
from jax.sharding import PartitionSpec as P

RANK = 8
DP = ("dp_0", "dp_1")
DP_TP = ("dp_0", "dp_1", "tp")


def by_axis(x, axes):
    for axis in axes:
        x = lax.psum(x, axis)
    return x


def on_device(gradients, right_factor, weights_before, momentum):
    own_grads = gradients[0]
    part_left = jnp.einsum(
        "liw,lwr->lir",
        own_grads,
        right_factor.astype(jnp.bfloat16),
        preferred_element_type=jnp.float32,
    )
    left = by_axis(part_left, DP)
    part_gram = jnp.einsum("lir,lis->lrs", left, left, precision=lax.Precision.HIGHEST)
    small_left = left.astype(jnp.bfloat16)
    part_right = jnp.einsum(
        "liw,lir->lwr", own_grads, small_left, preferred_element_type=jnp.float32
    )
    own_share = part_gram / lax.axis_size(DP)
    right, gram = lax.psum((part_right, own_share), DP_TP)
    gram = gram + 0.001 * jnp.mean(jnp.diagonal(gram, axis1=1, axis2=2), axis=1)[
        :, None, None
    ] * jnp.eye(RANK, dtype=jnp.float32)
    place = lax.axis_index(DP) * weights_before.shape[2]
    own_right = lax.dynamic_slice_in_dim(right, place, weights_before.shape[2], axis=1)
    root = jnp.linalg.cholesky(gram)
    half = lax.linalg.triangular_solve(
        root, jnp.swapaxes(own_right, 1, 2), left_side=True, lower=True
    )
    mixed = lax.linalg.triangular_solve(root, half, left_side=True, lower=True, transpose_a=True)
    change = jnp.einsum(
        "lir,lrw->liw", left, mixed, precision=lax.Precision.HIGHEST
    ) / lax.axis_size(DP)
    new_momentum = 0.9 * momentum + change
    new_weights = weights_before - 0.02 * new_momentum
    new_basis = right * lax.rsqrt(jnp.mean(right * right, axis=(1, 2), keepdims=True) + 1e-12)
    return (new_weights, new_basis, new_momentum)


def solution(mesh):
    split = Mesh(mesh.devices.reshape(4, 2, mesh.shape["tp"]), ("dp_0", "dp_1", "tp"))
    in_specs = (P(DP, None, "tp", None), P(), P(None, "tp", DP), P(None, "tp", DP))
    out_specs = (P(None, "tp", DP), P(), P(None, "tp", DP))
    return jax.shard_map(
        on_device, mesh=split, in_specs=in_specs, out_specs=out_specs, check_vma=False
    )
```

profile of v0, /device:TPU:1, one launch (start us, length us, event | category | flops | bytes accessed | tf_op | source)
XLA Modules:
  0.0 189.7 jit_solution(8125592697090335394)
XLA Ops:
  7.2 0.0 copy-start
  7.2 0.0 all-reduce.2.cloned.1.call-start
  7.2 1.2 copy-done
  8.4 1.3 fusion.3
  9.7 0.0 copy-start.2
  9.7 0.0 copy-start.3
  9.7 14.5 %psum.28 = f32[4,192,8]{1,2,0:T(8,128)S(1)} all-reduce(f32[4,192,8]{1,2,0:T(8,128)S(1)} %fusion.3), channel_id=1, replica_groups=mesh['dp_0'=4,'dp_1'=2,'tp'=16] {'dp_0'}, use_global_device_ids=true, to_apply=%region_0.0 | all-reduce | flops 6144 | bytes 49152 | tf_op jit(solution)/shard_map/psum | solution.py:14
  24.3 6.4 %psum.29 = f32[4,192,8]{1,2,0:T(8,128)S(1)} all-reduce(f32[4,192,8]{1,2,0:T(8,128)S(1)} %psum.28), channel_id=1, replica_groups=mesh['dp_0'=4,'dp_1'=2,'tp'=16] {'dp_1'}, use_global_device_ids=true, to_apply=%region_1.0 | all-reduce | flops 6144 | bytes 49152 | tf_op jit(solution)/shard_map/psum | solution.py:14
  30.6 0.9 fusion.5
  31.5 0.0 all-reduce.2.cloned.1.call-update
  31.6 0.2 convolution_multiply_fusion.1
  31.8 0.1 copy.13
  31.8 71.2 %psum.30 = f32[4,8,8]{1,2,0:T(8,128)S(1)} all-reduce(f32[4,8,8]{1,2,0:T(8,128)S(1)} %convolution_multiply_fusion.1), channel_id=1, replica_groups=mesh['dp_0'=4,'dp_1'=2,'tp'=16] {'dp_0','dp_1','tp'}, use_global_device_ids=true, to_apply=%region_2.0 | all-reduce | flops 256 | bytes 2048 | tf_op jit(solution)/shard_map/psum | solution.py:33
  103.0 0.1 copy.12
  103.2 0.6 gather_fusion
  103.8 0.1 multiply_add_fusion
  103.8 0.1 copy.14
  103.9 0.1 fusion.13
  104.0 2.9 %custom-call.9 = f32[4,8,8]{2,1,0:T(8,128)S(1)} custom-call(f32[4,8,8]{2,1,0:T(8,128)S(1)} %fusion.13), custom_call_target="Cholesky" | custom-call | tf_op jit(solution)/shard_map/jit(cholesky)/cholesky | solution.py:39
  106.9 0.1 select_reduce_fusion
  106.9 0.1 compare_reduce_fusion
  107.1 0.1 select_bitcast_fusion
  107.1 2.5 %custom-call.10 = f32[4,1,8,8]{2,3,1,0:T(8,128)S(1)} custom-call(f32[4,1,8,8]{3,2,1,0:T(8,128)S(1)} %select_bitcast_fusion), custom_call_target="InvertDiagBlocksLowerTriangular" | custom-call | tf_op jit(solution)/shard_map/triangular_solve | solution.py:43
  109.7 68.5 %all-reduce.2.cloned.1.call-done = f32[4,768,8]{1,2,0:T(8,128)} async-done(((f32[4,768,8]{1,2,0:T(8,128)}), f32[4,768,8]{1,2,0:T(8,128)}) %all-reduce.2.cloned.1.call-update) | async-done | bytes 98320 | tf_op jit(solution)/shard_map/psum | solution.py:33
  178.2 0.0 copy-start.1
  178.2 1.1 multiply_reduce_fusion
  179.2 1.0 fusion.11
  180.3 0.2 fusion.9
  180.4 0.0 copy-done.2
  180.4 0.0 copy-done.3
  180.4 1.7 multiply_subtract_fusion
  182.1 0.0 copy-done.1
  182.1 0.7 broadcast_multiply_fusion
  (7 shorter events, 0.1 us)
Async XLA Ops:
  7.2 1.3 copy-start
  7.2 171.0 %all-reduce.2.cloned.1.call-start = ((), (), s32[]{:S(2)}) async-start(), calls=%async_computation | async-start | bytes 196608 | tf_op jit(solution)/shard_map/psum | solution.py:33
  9.7 170.7 %copy-start.2 = (f32[4,192,96]{2,1,0:T(8,128)S(1)}, f32[4,192,96]{2,1,0:T(8,128)}, u32[]{:S(2)}) copy-start(f32[4,192,96]{2,1,0:T(8,128)} %param.6) | copy-start | bytes 884740
  9.7 170.7 %copy-start.3 = (f32[4,192,96]{2,1,0:T(8,128)S(1)}, f32[4,192,96]{2,1,0:T(8,128)}, u32[]{:S(2)}) copy-start(f32[4,192,96]{2,1,0:T(8,128)} %param.7) | copy-start | bytes 884740
  178.2 4.0 %copy-start.1 = (f32[4,768,8]{1,2,0:T(8,128)S(1)}, f32[4,768,8]{1,2,0:T(8,128)}, u32[]{:S(2)}) copy-start(f32[4,768,8]{1,2,0:T(8,128)} %all-reduce.2.cloned.1.call-done) | copy-start | bytes 294916
Sparse Core Ops, SparseCore 0:
  31.7 146.4 all-reduce.1
where the time goes:
time: 190 us
  blocking collectives  92.1 us (48%)
  waiting for transfers between devices  68.5 us (36%)
  between operations  14.1 us (7%)
  other arithmetic  7.66 us (4%)
  matrix products  5.23 us (3%)
  local copies, waits for them, and re-layouts  2.08 us (1%)
    psum x1, blocking collectives, on_device(): right, gram = lax.psum((part_right, own_share), DP_TP)  71.2 us
    psum x1, waiting for transfers between devices, on_device(): right, gram = lax.psum((part_right, own_share), DP_TP)  68.5 us
    psum x2, blocking collectives, by_axis(): x = lax.psum(x, axis)  20.9 us
  transfers between devices with their start and end apart: 1, of which 1 were waited for; matrix products, arithmetic and copies ran while one was open for 4% of the time, Pallas kernels for 0%

commit v1 on v0

--- a/solution.py
+++ b/solution.py
@@ -11,7 +11,7 @@
 
 def by_axis(x, axes):
     for axis in axes:
-        x = lax.psum(x, axis)
+        x = jnp.sum(lax.all_gather(x, axis), axis=0)
     return x
 
 

time: 190 us -> 183 us (0.963)
  blocking collectives: 92.1 us -> 84.2 us
    psum x2 -> x0, blocking collectives: 20.9 us -> none  [by_axis(): x = lax.psum(x, axis)]
    all_gather x0 -> x2, blocking collectives: none -> 14.1 us  [by_axis(): x = jnp.sum(lax.all_gather(x, axis), axis=0)]
where the time goes in v1:
time: 183 us
  blocking collectives  84.2 us (46%)
  waiting for transfers between devices  69.2 us (38%)
  between operations  14.1 us (8%)
  other arithmetic  7.68 us (4%)
  matrix products  5.22 us (3%)
  local copies, waits for them, and re-layouts  2.08 us (1%)
    psum x1, blocking collectives, on_device(): right, gram = lax.psum((part_right, own_share), DP_TP)  70.1 us
    psum x1, waiting for transfers between devices, on_device(): right, gram = lax.psum((part_right, own_share), DP_TP)  69.2 us
    all_gather x2, blocking collectives, by_axis(): x = jnp.sum(lax.all_gather(x, axis), axis=0)  14.1 us
  transfers between devices with their start and end apart: 1, of which 1 were waited for; matrix products, arithmetic and copies ran while one was open for 4% of the time, Pallas kernels for 0%

profile of v1, /device:TPU:1, one launch (start us, length us, event | category | flops | bytes accessed | tf_op | source)
XLA Modules:
  0.0 182.5 jit_solution(17034316184257275074)
XLA Ops:
  7.2 0.0 copy-start
  7.2 0.0 all-reduce.2.cloned.1.call-start
  7.2 1.2 copy-done
  8.4 1.3 fusion.3
  9.7 10.6 %all-gather = f32[16,192,8]{1,2,0:T(8,128)S(1)} all-gather(f32[4,192,8]{1,2,0:T(8,128)S(1)} %fusion.3), channel_id=2, replica_groups=mesh['dp_0'=4,'dp_1'=2,'tp'=16] {'dp_0'}, dimensions={0}, use_global_device_ids=true | all-gather | bytes 122880 | tf_op jit(solution)/shard_map/all_gather | solution.py:14
  20.3 0.0 copy-start.2
  20.3 0.0 copy-start.3
  20.3 3.6 %all-gather.1 = f32[8,192,8]{1,2,0:T(8,128)S(1)} all-gather(f32[4,192,8]{1,2,0:T(8,128)S(1)} %reduce_sum.36), channel_id=3, replica_groups=mesh['dp_0'=4,'dp_1'=2,'tp'=16] {'dp_1'}, dimensions={0}, use_global_device_ids=true | all-gather | bytes 73728 | tf_op jit(solution)/shard_map/all_gather | solution.py:14
  23.9 0.9 fusion.5
  24.8 0.0 all-reduce.2.cloned.1.call-update
  24.9 0.2 convolution_multiply_fusion.1
  25.0 0.1 copy.17
  25.1 70.1 %psum.14 = f32[4,8,8]{1,2,0:T(8,128)S(1)} all-reduce(f32[4,8,8]{1,2,0:T(8,128)S(1)} %convolution_multiply_fusion.1), channel_id=1, replica_groups=mesh['dp_0'=4,'dp_1'=2,'tp'=16] {'dp_0','dp_1','tp'}, use_global_device_ids=true, to_apply=%region_2.0 | all-reduce | flops 256 | bytes 2048 | tf_op jit(solution)/shard_map/psum | solution.py:33
  95.2 0.1 copy.16
  95.3 0.6 gather_fusion
  95.9 0.1 multiply_add_fusion
  96.0 0.1 copy.18
  96.1 0.1 fusion.13
  96.1 2.9 %custom-call.9 = f32[4,8,8]{2,1,0:T(8,128)S(1)} custom-call(f32[4,8,8]{2,1,0:T(8,128)S(1)} %fusion.13), custom_call_target="Cholesky" | custom-call | tf_op jit(solution)/shard_map/jit(cholesky)/cholesky | solution.py:39
  99.0 0.1 select_reduce_fusion
  99.1 0.1 compare_reduce_fusion
  99.2 0.1 select_bitcast_fusion
  99.3 2.5 %custom-call.10 = f32[4,1,8,8]{2,3,1,0:T(8,128)S(1)} custom-call(f32[4,1,8,8]{3,2,1,0:T(8,128)S(1)} %select_bitcast_fusion), custom_call_target="InvertDiagBlocksLowerTriangular" | custom-call | tf_op jit(solution)/shard_map/triangular_solve | solution.py:43
  101.8 69.2 %all-reduce.2.cloned.1.call-done = f32[4,768,8]{1,2,0:T(8,128)} async-done(((f32[4,768,8]{1,2,0:T(8,128)}), f32[4,768,8]{1,2,0:T(8,128)}) %all-reduce.2.cloned.1.call-update) | async-done | bytes 98320 | tf_op jit(solution)/shard_map/psum | solution.py:33
  171.0 0.0 copy-start.1
  171.0 1.1 multiply_reduce_fusion
  172.1 1.0 fusion.11
  173.1 0.2 fusion.9
  173.2 0.0 copy-done.2
  173.2 0.0 copy-done.3
  173.3 1.7 multiply_subtract_fusion
  175.0 0.0 copy-done.1
  175.0 0.7 broadcast_multiply_fusion
  (9 shorter events, 0.1 us)
Async XLA Ops:
  7.2 1.3 copy-start
  7.2 163.8 %all-reduce.2.cloned.1.call-start = ((), (), s32[]{:S(2)}) async-start(), calls=%async_computation | async-start | bytes 196608 | tf_op jit(solution)/shard_map/psum | solution.py:33
  20.3 153.0 %copy-start.2 = (f32[4,192,96]{2,1,0:T(8,128)S(1)}, f32[4,192,96]{2,1,0:T(8,128)}, u32[]{:S(2)}) copy-start(f32[4,192,96]{2,1,0:T(8,128)} %param.6) | copy-start | bytes 884740
  20.3 153.0 %copy-start.3 = (f32[4,192,96]{2,1,0:T(8,128)S(1)}, f32[4,192,96]{2,1,0:T(8,128)}, u32[]{:S(2)}) copy-start(f32[4,192,96]{2,1,0:T(8,128)} %param.7) | copy-start | bytes 884740
  171.0 4.0 %copy-start.1 = (f32[4,768,8]{1,2,0:T(8,128)S(1)}, f32[4,768,8]{1,2,0:T(8,128)}, u32[]{:S(2)}) copy-start(f32[4,768,8]{1,2,0:T(8,128)} %all-reduce.2.cloned.1.call-done) | copy-start | bytes 294916
Sparse Core Ops, SparseCore 0:
  24.9 145.9 all-reduce.1
